TPU v7x, 32 devices: a whole 2x2x4 slice. The times are simulated.
32 devices in a mesh: dp: 16 (over z, x, core), head: 2 (over y).
Axes of the slice: x: 2, y: 2, z: 4, core: 2. Of those that a mesh axis runs over, the one named last changes fastest.
Arguments:
- layer_input: bfloat16 [16384, 768], P('dp', 'head'), may hold values from -6 to 6
- first_gain: float32 [768], replicated, may hold values from 0.5 to 1.5
- first_shift: float32 [768], replicated, may hold values from -3 to 3
- qkv_weight: bfloat16 [3, 768, 768], P(None, None, 'head'), may hold values from -0.5 to 0.5
- out_weight: bfloat16 [768, 768], P('head'), may hold values from -0.875 to 0.875
- second_gain: float32 [768], replicated, may hold values from 0.5 to 1.5
- second_shift: float32 [768], replicated, may hold values from -3 to 3
- up_weight: bfloat16 [768, 3072], P(None, 'head'), may hold values from -0.21875 to 0.21875
- down_weight: bfloat16 [3072, 768], P('head'), may hold values from -0.15625 to 0.15625
- segment_ids: int32 [16384], P('dp'), may hold values from 0 to 4, as said below
- pad_mask: int32 [16384], P('dp'), may hold values from 0 to 1, as said below
- cluster_ids: int32 [12, 16384], P('head', 'dp'), may hold values from 0 to 99, as said below
- output_grad: bfloat16 [16384, 768], P('dp', 'head'), may hold values from -6 to 6
Outputs:
- layer_output: bfloat16 [16384, 768], P('dp', 'head')
- input_grad: bfloat16 [16384, 768], P('dp', 'head')
- qkv_grad: float32 [3, 768, 768], P(None, None, 'head')
- mix_weight_grad: float32 [768, 768], P('head')
- up_grad: float32 [768, 3072], P(None, 'head')
- down_grad: float32 [3072, 768], P('head')
- first_gain_grad: float32 [768], replicated
- first_shift_grad: float32 [768], replicated
- second_gain_grad: float32 [768], replicated
- second_shift_grad: float32 [768], replicated
Inputs may be any that keep to these rules, and one draw needn't show every extreme that they name: `segment_ids`: never falling within a sequence of 1024 tokens; 4 documents numbered 0 .. 3, each of 128 tokens or more, then one or more padding tokens numbered 4 at the sequence's end. `pad_mask`: 1 exactly on the tokens of documents, 0 on padding. `cluster_ids`: in each head and sequence every cluster holds at least one token with pad_mask 1, and all such tokens of a cluster lie in one document.
All inputs are finite; a program needn't handle non-finite values.
Results may differ from a plain program's by a relative error of at most 0.015.
The roundings to bfloat16 on the way count: a program that leaves them out, or rounds other values in their place, can miss the bound.
Values may be sent and summed in bfloat16 or wider, within the bound.
A program may use at most 128 MiB of HBM per device.

v0:
```python
import jax
import jax.numpy as jnp
from jax import lax
from jax.sharding import PartitionSpec as P

HDIM = 64
CLUST = 100
epsilon = 1e-05
far_below = -1e30
highest = lax.Precision.HIGHEST


def norm_parts(values):
    row_mean = jnp.mean(values, axis=-1, keepdims=True)
    centred = values - row_mean
    variance = jnp.mean(centred * centred, axis=-1, keepdims=True)
    row_scale = lax.rsqrt(variance + epsilon)
    return (centred * row_scale, row_scale)


def norm_back(upstream, normal, row_scale):
    first_term = jnp.mean(upstream, axis=-1, keepdims=True)
    second_term = jnp.mean(upstream * normal, axis=-1, keepdims=True)
    return row_scale * (upstream - first_term - normal * second_term)


def attention_parts(query, keys, segment_ids, pad_mask, cluster_ids):
    live_rows = (pad_mask > 0).astype(jnp.float32)
    labels = jnp.arange(CLUST, dtype=jnp.int32)
    member = (cluster_ids[:, None, :] == labels[None, :, None]).astype(jnp.float32) * live_rows[
        None, None, :
    ]
    counts = jnp.sum(member, axis=-1)
    member_low = member.astype(jnp.bfloat16)
    centre = (
        jnp.einsum("hcs,she->hce", member_low, query, preferred_element_type=jnp.float32)
        / counts[:, :, None]
    ).astype(jnp.bfloat16)
    seg_float = segment_ids.astype(jnp.float32)
    doc_owner = jnp.einsum("hcs,s->hc", member, seg_float, precision=highest) / counts
    allowed = (jnp.abs(doc_owner[:, :, None] - seg_float[None, None, :]) < 0.5) & (
        pad_mask[None, None, :] > 0
    )
    scores = jnp.einsum(
        "hce,she->hcs", centre, keys, preferred_element_type=jnp.float32
    ) * HDIM ** (-0.5)
    masked = jnp.where(allowed, scores, far_below)
    return (member, member_low, counts, centre, masked)


def shards(
    layer_input,
    first_gain,
    first_shift,
    qkv_weight,
    out_weight,
    second_gain,
    second_shift,
    up_weight,
    down_weight,
    segment_ids,
    pad_mask,
    cluster_ids,
    output_grad,
):
    tokens, local_width = layer_input.shape
    head_count = cluster_ids.shape[0]
    score_scale = HDIM ** (-0.5)
    start = lax.axis_index("head") * local_width
    whole_in = lax.all_gather(layer_input, "head", axis=1, tiled=True).astype(jnp.float32)
    first_hat, first_scale = norm_parts(whole_in)
    normed = (first_hat * first_gain + first_shift).astype(jnp.bfloat16)
    projected = jnp.einsum(
        "td,ide->ite", normed, qkv_weight, preferred_element_type=jnp.float32
    ).astype(jnp.bfloat16)
    head_parts = projected.reshape(3, tokens, head_count, HDIM)
    query, keys, values = (head_parts[0], head_parts[1], head_parts[2])
    member, member_low, counts, centre, masked = attention_parts(
        query, keys, segment_ids, pad_mask, cluster_ids
    )
    row_top = jnp.max(masked, axis=-1, keepdims=True)
    log_total = row_top + jnp.log(jnp.sum(jnp.exp(masked - row_top), axis=-1, keepdims=True))
    weights = jnp.exp(masked - log_total).astype(jnp.bfloat16)
    centre_out = jnp.einsum(
        "hcs,she->hce", weights, values, preferred_element_type=jnp.float32
    ).astype(jnp.bfloat16)
    mixture = (
        jnp.einsum("hcs,hce->she", member_low, centre_out, preferred_element_type=jnp.float32)
        .astype(jnp.bfloat16)
        .reshape(tokens, local_width)
    )
    branch_part = jnp.dot(mixture, out_weight, preferred_element_type=jnp.float32)
    branch = lax.psum_scatter(
        branch_part.astype(jnp.bfloat16), "head", scatter_dimension=1, tiled=True
    ).astype(jnp.float32)
    residual = layer_input.astype(jnp.float32) + branch
    whole_res = lax.all_gather(residual.astype(jnp.bfloat16), "head", axis=1, tiled=True).astype(
        residual.dtype
    )
    second_hat, second_scale = norm_parts(whole_res)
    second = (second_hat * second_gain + second_shift).astype(jnp.bfloat16)
    hidden = jnp.dot(second, up_weight, preferred_element_type=jnp.float32)
    activated, gelu_back = jax.vjp(jax.nn.gelu, hidden)
    activated = activated.astype(jnp.bfloat16)
    ffn_part = jnp.dot(activated, down_weight, preferred_element_type=jnp.float32)
    ffn_out = lax.psum_scatter(
        ffn_part.astype(jnp.bfloat16), "head", scatter_dimension=1, tiled=True
    ).astype(jnp.float32)
    layer_output = (residual + ffn_out).astype(jnp.bfloat16)
    whole_grad = lax.all_gather(output_grad, "head", axis=1, tiled=True)
    down_grad = jnp.einsum("tf,td->fd", activated, whole_grad, preferred_element_type=jnp.float32)
    act_grad = jnp.einsum("td,fd->tf", whole_grad, down_weight, preferred_element_type=jnp.float32)
    hidden_grad = gelu_back(act_grad)[0].astype(jnp.bfloat16)
    up_grad = jnp.einsum("td,tf->df", second, hidden_grad, preferred_element_type=jnp.float32)
    second_part = jnp.einsum(
        "tf,df->td", hidden_grad, up_weight, preferred_element_type=jnp.float32
    )
    second_back = lax.psum(second_part, "head")
    second_gain_grad = jnp.sum(second_back * second_hat, axis=0)
    second_shift_grad = jnp.sum(second_back, axis=0)
    residual_grad = whole_grad.astype(jnp.float32) + norm_back(
        second_back * second_gain, second_hat, second_scale
    )
    branch_grad = residual_grad.astype(jnp.bfloat16)
    mix_weight_grad = jnp.einsum(
        "te,td->ed", mixture, branch_grad, preferred_element_type=jnp.float32
    )
    mixture_grad = jnp.einsum(
        "td,ed->te", branch_grad, out_weight, preferred_element_type=jnp.float32
    ).reshape(tokens, head_count, HDIM)
    centre_out_grad = jnp.einsum("hcs,she->hce", member, mixture_grad, precision=highest).astype(
        jnp.bfloat16
    )
    probs = jnp.exp(masked - log_total)
    prob_grad = jnp.einsum(
        "hce,she->hcs", centre_out_grad, values, preferred_element_type=jnp.float32
    )
    value_grad = jnp.einsum(
        "hcs,hce->she", weights, centre_out_grad, preferred_element_type=jnp.float32
    )
    score_grad = (probs * (prob_grad - jnp.sum(prob_grad * probs, axis=-1, keepdims=True))).astype(
        jnp.bfloat16
    )
    centre_grad = (
        jnp.einsum("hcs,she->hce", score_grad, keys, preferred_element_type=jnp.float32)
        * score_scale
    )
    key_grad = (
        jnp.einsum("hcs,hce->she", score_grad, centre, preferred_element_type=jnp.float32)
        * score_scale
    )
    query_grad = jnp.einsum(
        "hcs,hce->she", member, centre_grad / counts[:, :, None], precision=highest
    )
    proj_grad = (
        jnp.stack([query_grad, key_grad, value_grad])
        .reshape(3, tokens, local_width)
        .astype(jnp.bfloat16)
    )
    qkv_grad = jnp.einsum("td,ite->ide", normed, proj_grad, preferred_element_type=jnp.float32)
    first_part = jnp.einsum(
        "ite,ide->td", proj_grad, qkv_weight, preferred_element_type=jnp.float32
    )
    first_back = lax.psum(first_part.astype(jnp.bfloat16), "head").astype(jnp.float32)
    first_gain_grad = jnp.sum(first_back * first_hat, axis=0)
    first_shift_grad = jnp.sum(first_back, axis=0)
    input_full = residual_grad + norm_back(first_back * first_gain, first_hat, first_scale)
    input_grad = lax.dynamic_slice_in_dim(input_full, start, local_width, 1).astype(jnp.bfloat16)
    summed = lax.psum(
        (
            qkv_grad,
            mix_weight_grad,
            up_grad,
            down_grad,
            first_gain_grad,
            first_shift_grad,
            second_gain_grad,
            second_shift_grad,
        ),
        "dp",
    )
    (
        qkv_total,
        mix_total,
        up_total,
        down_total,
        first_gain_total,
        first_shift_total,
        second_gain_total,
        second_shift_total,
    ) = summed
    return (
        layer_output,
        input_grad,
        qkv_total,
        mix_total,
        up_total,
        down_total,
        first_gain_total,
        first_shift_total,
        second_gain_total,
        second_shift_total,
    )


def solution(mesh):
    placed = (
        P("dp", "head"),
        P(),
        P(),
        P(None, None, "head"),
        P("head", None),
        P(),
        P(),
        P(None, "head"),
        P("head", None),
        P("dp"),
        P("dp"),
        P("head", "dp"),
        P("dp", "head"),
    )
    return jax.shard_map(
        shards,
        mesh=mesh,
        in_specs=placed,
        out_specs=(
            P("dp", "head"),
            P("dp", "head"),
            P(None, None, "head"),
            P("head", None),
            P(None, "head"),
            P("head", None),
            P(),
            P(),
            P(),
            P(),
        ),
        check_vma=False,
    )
```

profile of v0, /device:TPU:0, one launch (start us, length us, event | category | flops | bytes accessed | tf_op | source)
XLA Modules:
  0.0 614.1 jit_solution(7935351262349309971)
XLA Ops:
  13.8 25.7 %all-gather.4.cloned.1.call-done = bf16[1024,768]{1,0:T(8,128)(2,1)} async-done(((bf16[1024,384]{1,0:T(8,128)(2,1)}), bf16[1024,768]{1,0:T(8,128)(2,1)}) %all-gather.4.cloned.1.call-update) | async-done | bytes 1572880 | tf_op jit(solution)/shard_map/all_gather | solution.py:70
  42.0 3.8 convert_bitcast_fusion
  50.5 3.8 fusion.40
  54.3 3.5 convolution_convert_fusion
  61.1 25.5 %reduce-scatter.7.cloned.1.call-done = bf16[384,1024]{1,0:T(8,128)(2,1)} async-done(((bf16[768,1024]{1,0:T(8,128)(2,1)}), bf16[384,1024]{1,0:T(8,128)(2,1)}) %reduce-scatter.7.cloned.1.call-update) | async-done | bytes 786448
  91.7 23.7 %all-gather.8.cloned.1.call-done = bf16[1024,768]{1,0:T(8,128)(2,1)} async-done(((bf16[1024,384]{1,0:T(8,128)(2,1)}), bf16[1024,768]{1,0:T(8,128)(2,1)}) %all-gather.8.cloned.1.call-update) | async-done | bytes 1572880 | tf_op jit(solution)/shard_map/all_gather | solution.py:110
  115.4 7.4 %fusion.92 = f32[1024,1536]{1,0:T(8,128)} fusion(bf16[1024,768]{1,0:T(8,128)(2,1)} %all-gather.8.cloned.1.call-done, bf16[1536,768]{1,0:T(8,128)(2,1)} %param.21), kind=kOutput, calls=%fused_computation.127 | convolution fusion | flops 2415919104 | bytes 10223616 | tf_op jit(solution)/shard_map/td,fd->tf/dot_general | solution.py:112
  122.9 21.8 %all-gather.6.cloned.1.call-done = bf16[1024,768]{1,0:T(8,128)(2,1)} async-done(((bf16[1024,384]{1,0:T(8,128)(2,1)}), bf16[1024,768]{1,0:T(8,128)(2,1)}) %all-gather.6.cloned.1.call-update) | async-done | bytes 1572880 | tf_op jit(solution)/shard_map/all_gather | solution.py:97
  147.2 9.7 %fusion.6 = (bf16[1024,1536]{1,0:T(8,128)(2,1)S(1)}, f32[1024,1536]{1,0:T(8,128)}) fusion(f32[1024,1536]{1,0:T(8,128)} %fusion.92, bf16[768,1536]{1,0:T(8,128)(2,1)S(1)} %copy-done, bf16[1024,768]{1,0:T(8,128)(2,1)S(1)} %copy-done.7, f32[768]{0:T(1024)S(1)} %copy-done.28, f32[768]{0:T(1024)S(1)} %copy-done.26, f32[1024]{0:T(1024)S(1)} %add_rsqrt_fusion, ...), kind=kOutput, calls=%fused_computation.8 | convolution fusion | flops 2452094976 | bytes 19675136 | tf_op jit(solution)/shard_map/dot_general | solution.py:102
  158.6 4.3 fusion.93
  163.0 7.2 %convolution_convert_fusion.1 = bf16[1024,768]{1,0:T(8,128)(2,1)S(1)} fusion(bf16[1536,768]{1,0:T(8,128)(2,1)} %param.21, f32[1024,1536]{1,0:T(8,128)} %get-tuple-element.56), kind=kOutput, calls=%fused_computation.60 | convolution fusion | flops 2430861312 | bytes 10223616 | tf_op jit(solution)/shard_map/dot_general | solution.py:105
  171.9 9.2 %fusion.86 = f32[1536,768]{1,0:T(8,128)} fusion(bf16[1024,768]{1,0:T(8,128)(2,1)} %all-gather.8.cloned.1.call-done, f32[1024,1536]{1,0:T(8,128)} %get-tuple-element.56), kind=kOutput, calls=%fused_computation.123 | convolution fusion | flops 2430074880 | bytes 12582912 | tf_op jit(solution)/shard_map/tf,td->fd/dot_general | solution.py:111
  181.1 67.8 %all-reduce.6.cloned.1.call-done = f32[1024,768]{1,0:T(8,128)} async-done(((f32[1024,768]{1,0:T(8,128)}), f32[1024,768]{1,0:T(8,128)}) %all-reduce.6.cloned.1.call-update) | async-done | bytes 3145744 | tf_op jit(solution)/shard_map/psum | solution.py:118
  248.9 3.4 fusion.27
  273.8 5.3 bitcast_convert_fusion
  279.2 6.8 %fusion.82 = f32[768,1536]{1,0:T(8,128)} fusion(bf16[1024,1536]{1,0:T(8,128)(2,1)} %copy-done.30, bf16[1024,768]{1,0:T(8,128)(2,1)S(1)} %copy-done.8, f32[768]{0:T(1024)S(1)} %copy-done.28, f32[768]{0:T(1024)S(1)} %copy-done.26, f32[1024]{0:T(1024)S(1)} %add_rsqrt_fusion, f32[1024]{0:T(1024)S(1)} %broadcast_multiply_fusion.4), kind=kOutput, calls=%fused_computation.121 | convolution fusion | flops 2420637696 | bytes 9451520 | tf_op jit(solution)/shard_map/td,tf->df/dot_general | solution.py:114
  288.5 4.3 convolution_bitcast_fusion
  297.5 33.5 %all-reduce.8.cloned.1.call-done = bf16[1024,768]{1,0:T(8,128)(2,1)} async-done(((bf16[1024,768]{1,0:T(8,128)(2,1)}), bf16[1024,768]{1,0:T(8,128)(2,1)}) %all-reduce.8.cloned.1.call-update) | async-done | bytes 1572880 | tf_op jit(solution)/shard_map/psum | solution.py:164
  331.0 4.6 fusion.30
  335.6 64.1 %all-reduce = (f32[768]{0:T(1024)}, f32[768]{0:T(1024)}, f32[768]{0:T(1024)}, f32[768]{0:T(1024)}) all-reduce(f32[768]{0:T(1024)S(1)} %get-tuple-element.32, f32[768]{0:T(1024)S(1)} %get-tuple-element.37, f32[768]{0:T(1024)S(1)} %get-tuple-element.30, f32[768]{0:T(1024)S(1)} %get-tuple-element.35), channel_id=1, replica_groups=mesh['dp'=16,'head'=2] {'dp'}, use_global_device_ids=true, to_apply=%region_21.22 | all-reduce | flops 3072 | bytes 24576 | tf_op jit(solution)/shard_map/psum | solution.py:169
  399.7 3.8 fusion.36
  403.4 189.6 %all-reduce.10.cloned.1.call-done = (f32[3,768,384]{1,2,0:T(8,128)}, f32[384,768]{1,0:T(8,128)}, f32[768,1536]{1,0:T(8,128)}, f32[1536,768]{1,0:T(8,128)}) async-done(((f32[3,768,384]{1,2,0:T(8,128)}, f32[384,768]{1,0:T(8,128)}, f32[768,1536]{1,0:T(8,128)}, f32[1536,768]{1,0:T(8,128)}), (f32[3,768,384]{1,2,0:T(8,128)}, f32[384,768]{1,0:T(8,128)}, f32[768,1536]{1,0:T(8,128)}, ...) | async-done | bytes 14155792 | tf_op jit(solution)/shard_map/psum | solution.py:169
  593.0 5.2 copy.34
  599.3 5.5 copy.50
  (126 shorter events, 59.8 us)
Async XLA Ops:
  7.2 140.0 %copy-start = (bf16[768,1536]{1,0:T(8,128)(2,1)S(1)}, bf16[768,1536]{1,0:T(8,128)(2,1)}, u32[]{:S(2)}) copy-start(bf16[768,1536]{1,0:T(8,128)(2,1)} %param.20) | copy-start | bytes 7077892
  7.2 32.3 %all-gather.4.cloned.1.call-start = ((), (), s32[]{:S(2)}) async-start(), calls=%async_computation.2 | async-start | bytes 2359296 | tf_op jit(solution)/shard_map/all_gather | solution.py:70
  7.9 34.1 %copy-start.27 = (f32[768]{0:T(1024)S(1)}, f32[768]{0:T(1024)}, u32[]{:S(2)}) copy-start(f32[768]{0:T(1024)} %param.14) | copy-start | bytes 9220
  7.9 34.1 %copy-start.29 = (f32[768]{0:T(1024)S(1)}, f32[768]{0:T(1024)}, u32[]{:S(2)}) copy-start(f32[768]{0:T(1024)} %param.15) | copy-start | bytes 9220
  7.9 78.7 %reduce-scatter.7.cloned.1.call-start = ((), (), s32[]{:S(2)}) async-start(), calls=%async_computation.7 | async-start | bytes 2359296
  46.1 4.4 copy-start.15
  60.3 28.6 %copy-start.12 = (bf16[1024,384]{1,0:T(8,128)(2,1)S(1)}, bf16[1024,384]{1,0:T(8,128)(2,1)}, u32[]{:S(2)}) copy-start(bf16[1024,384]{1,0:T(8,128)(2,1)} %param.13) | copy-start | bytes 2359300
  60.4 55.1 %all-gather.8.cloned.1.call-start = ((), (), s32[]{:S(2)}) async-start(), calls=%async_computation.4 | async-start | bytes 2359296 | tf_op jit(solution)/shard_map/all_gather | solution.py:110
  61.1 83.5 %all-gather.6.cloned.1.call-start = ((), (), s32[]{:S(2)}) async-start(), calls=%async_computation.3 | async-start | bytes 2359296 | tf_op jit(solution)/shard_map/all_gather | solution.py:97
  91.2 157.7 %all-reduce.6.cloned.1.call-start = ((), (), s32[]{:S(2)}) async-start(), calls=%async_computation.5 | async-start | bytes 6291456 | tf_op jit(solution)/shard_map/psum | solution.py:118
  122.9 24.3 %copy-start.26 = (f32[768]{0:T(1024)S(1)}, f32[768]{0:T(1024)}, u32[]{:S(2)}) copy-start(f32[768]{0:T(1024)} %param.18) | copy-start | bytes 9220
  122.9 24.3 %copy-start.28 = (f32[768]{0:T(1024)S(1)}, f32[768]{0:T(1024)}, u32[]{:S(2)}) copy-start(f32[768]{0:T(1024)} %param.19) | copy-start | bytes 9220
  162.9 129.9 %reduce-scatter.9.cloned.1.call-start = ((), (), s32[]{:S(2)}) async-start(), calls=%async_computation.8 | async-start | bytes 2359296
  171.9 77.0 %copy-start.8 = (bf16[1024,768]{1,0:T(8,128)(2,1)S(1)}, bf16[1024,768]{1,0:T(8,128)(2,1)}, u32[]{:S(2)}) copy-start(bf16[1024,768]{1,0:T(8,128)(2,1)} %all-gather.6.cloned.1.call-done) | copy-start | bytes 4718596
  171.9 159.1 %all-reduce.8.cloned.1.call-start = ((), (), s32[]{:S(2)}) async-start(), calls=%async_computation.6 | async-start | bytes 3145728 | tf_op jit(solution)/shard_map/psum | solution.py:164
  248.9 3.4 copy-start.16
  266.6 7.2 %copy-start.20 = (bf16[1,1024,384]{2,1,0:T(8,128)(2,1)S(1)}, bf16[1,1024,384]{2,1,0:T(8,128)(2,1)}, u32[]{:S(2)}) copy-start(bf16[1,1024,384]{2,1,0:T(8,128)(2,1)} %copy.32) | copy-start | bytes 2359300
  279.1 6.9 %copy-start.18 = (bf16[6,64,1024]{2,1,0:T(8,128)(2,1)S(1)}, bf16[6,64,1024]{2,1,0:T(8,128)(2,1)}, u32[]{:S(2)}) copy-start(bf16[6,64,1024]{2,1,0:T(8,128)(2,1)} %fusion.40) | copy-start | bytes 2359300
  279.1 313.9 %all-reduce.10.cloned.1.call-start = ((), (), s32[]{:S(2)}) async-start(), calls=%async_computation.9 | async-start | bytes 28311552 | tf_op jit(solution)/shard_map/psum | solution.py:169
  279.2 6.8 %copy-start.6 = (f32[1024,768]{1,0:T(8,128)S(1)}, f32[1024,768]{1,0:T(8,128)}, u32[]{:S(2)}) copy-start(f32[1024,768]{1,0:T(8,128)} %copy-done.5) | copy-start | bytes 9437188
  593.0 5.3 copy-start.17
  598.3 6.5 %slice-start = ((s8[4718592]{0:T(1024)(128)(4,1)}), s8[4194304]{0:T(1024)(128)(4,1)S(1)}, s32[]{:S(2)}) async-start(s8[4718592]{0:T(1024)(128)(4,1)} %bitcast.63), calls=%async_computation.10 | async-start | bytes 8388608
  599.3 5.5 slice-start.1
  599.3 7.7 %copy-start.1 = (bf16[768,1536]{1,0:T(8,128)(2,1)S(1)}, bf16[768,1536]{1,0:T(8,128)(2,1)}, u32[]{:S(2)}) copy-start(bf16[768,1536]{1,0:T(8,128)(2,1)} %param.20) | copy-start | bytes 7077892
  (17 other events, 34.2 us)
Sparse Core Ops, SparseCore 0:
  9.5 29.9 all-gather.3
  60.5 26.1 reduce-scatter.6
  88.2 27.1 all-gather.7
  117.4 27.1 all-gather.5
  163.0 85.8 all-reduce.5
  251.0 26.1 reduce-scatter.8
  279.5 51.5 all-reduce.7
  336.2 256.7 all-reduce.9
where the time goes:
time: 623 us; the launch traced here: 614 us
  waiting for transfers between devices  389 us (62%)
  matrix products  85.2 us (14%)
  blocking collectives  64.1 us (10%)
  local copies, waits for them, and re-layouts  34.1 us (5%)
  other arithmetic  26.2 us (4%)
  between operations  14.8 us (2%)
    psum x1, waiting for transfers between devices, shards(): lax.psum((qkv_grad, mix_weight_grad, up_grad, down_grad, first_gain_grad,...  190 us
    psum x1, waiting for transfers between devices, shards(): second_back = lax.psum(second_part, 'head')  67.8 us
    psum x1, blocking collectives, shards(): lax.psum((qkv_grad, mix_weight_grad, up_grad, down_grad, first_gain_grad,...  64.1 us
    psum x1, waiting for transfers between devices, shards(): lax.psum(first_part.astype(jnp.bfloat16), 'head').astype(jnp.float32)  33.5 us
    unnamed x74, local copies, waits for them, and re-layouts  29.2 us
    unnamed x10, waiting for transfers between devices  27 us
    all_gather x1, waiting for transfers between devices, shards(): lax.all_gather(layer_input, 'head', axis=1, tiled=True).astype(jnp.float32)  25.7 us
    all_gather x1, waiting for transfers between devices, shards(): whole_grad = lax.all_gather(output_grad, 'head', axis=1, tiled=True)  23.7 us
  transfers between devices with their start and end apart: 8, of which 7 were waited for; matrix products, arithmetic and copies ran while one was open for 15% of the time, Pallas kernels for 0%

commit v1 on v0

--- a/solution.py
+++ b/solution.py
@@ -161,7 +161,8 @@
     first_part = jnp.einsum(
         "ite,ide->td", proj_grad, qkv_weight, preferred_element_type=jnp.float32
     )
-    first_back = lax.psum(first_part.astype(jnp.bfloat16), "head").astype(jnp.float32)
+    test_the_pools = lambda piece_in: lax.all_gather(piece_in, "head").sum(axis=0)
+    first_back = test_the_pools(first_part.astype(jnp.bfloat16)).astype(jnp.float32)
     first_gain_grad = jnp.sum(first_back * first_hat, axis=0)
     first_shift_grad = jnp.sum(first_back, axis=0)
     input_full = residual_grad + norm_back(first_back * first_gain, first_hat, first_scale)

time: 623 us -> 616 us (0.989)
  waiting for transfers between devices: 389 us -> 374 us
    psum x1 -> x0, waiting for transfers between devices: 33.5 us -> none  [shards(): lax.psum(first_part.astype(jnp.bfloat16), 'head').astype(jnp.float32)]
    all_gather x0 -> x1, waiting for transfers between devices: none -> 17.3 us  [shards(): lax.all_gather(piece_in, 'head').sum(axis=0)]
    unnamed x74 -> x78, local copies, waits for them, and re-layouts: 29.2 us -> 32 us
  transfers between devices with their start and end apart: 8 -> 8, of which waited for: 7 -> 7; matrix products, arithmetic and copies ran while one was open for 15% -> 16% of each run, Pallas kernels for 0% -> 0%
where the time goes in v1:
time: 616 us; the launch traced here: 607 us
  waiting for transfers between devices  374 us (61%)
  matrix products  85.5 us (14%)
  blocking collectives  64.3 us (10%)
  local copies, waits for them, and re-layouts  36.8 us (6%)
  other arithmetic  30.1 us (5%)
  between operations  14.8 us (2%)
    psum x1, waiting for transfers between devices, shards(): lax.psum((qkv_grad, mix_weight_grad, up_grad, down_grad, first_gain_grad,...  185 us
    psum x1, waiting for transfers between devices, shards(): second_back = lax.psum(second_part, 'head')  73.7 us
    psum x1, blocking collectives, shards(): lax.psum((qkv_grad, mix_weight_grad, up_grad, down_grad, first_gain_grad,...  64.3 us
    unnamed x78, local copies, waits for them, and re-layouts  32 us
    unnamed x10, waiting for transfers between devices  27 us
    all_gather x1, waiting for transfers between devices, shards(): lax.all_gather(layer_input, 'head', axis=1, tiled=True).astype(jnp.float32)  25.7 us
    all_gather x1, waiting for transfers between devices, shards(): whole_grad = lax.all_gather(output_grad, 'head', axis=1, tiled=True)  23.7 us
    all_gather x1, waiting for transfers between devices, shards(): lax.all_gather(residual.astype(jnp.bfloat16), 'head', axis=1, tiled=True)  21.8 us
  transfers between devices with their start and end apart: 8, of which 7 were waited for; matrix products, arithmetic and copies ran while one was open for 16% of the time, Pallas kernels for 0%

profile of v1, /device:TPU:0, one launch (start us, length us, event | category | flops | bytes accessed | tf_op | source)
XLA Modules:
  0.0 607.1 jit_solution(6822943436890923195)
XLA Ops:
  13.8 25.7 %all-gather.6.cloned.1.call-done = bf16[1024,768]{1,0:T(8,128)(2,1)} async-done(((bf16[1024,384]{1,0:T(8,128)(2,1)}), bf16[1024,768]{1,0:T(8,128)(2,1)}) %all-gather.6.cloned.1.call-update) | async-done | bytes 1572880 | tf_op jit(solution)/shard_map/all_gather | solution.py:70
  42.0 3.8 convert_bitcast_fusion
  50.5 3.8 fusion.40
  54.3 3.5 convolution_convert_fusion
  61.1 25.5 %reduce-scatter.7.cloned.1.call-done = bf16[384,1024]{1,0:T(8,128)(2,1)} async-done(((bf16[768,1024]{1,0:T(8,128)(2,1)}), bf16[384,1024]{1,0:T(8,128)(2,1)}) %reduce-scatter.7.cloned.1.call-update) | async-done | bytes 786448
  91.7 23.7 %all-gather.10.cloned.1.call-done = bf16[1024,768]{1,0:T(8,128)(2,1)} async-done(((bf16[1024,384]{1,0:T(8,128)(2,1)}), bf16[1024,768]{1,0:T(8,128)(2,1)}) %all-gather.10.cloned.1.call-update) | async-done | bytes 1572880 | tf_op jit(solution)/shard_map/all_gather | solution.py:110
  115.4 7.4 %fusion.92 = f32[1024,1536]{1,0:T(8,128)} fusion(bf16[1024,768]{1,0:T(8,128)(2,1)} %all-gather.10.cloned.1.call-done, bf16[1536,768]{1,0:T(8,128)(2,1)} %param.21), kind=kOutput, calls=%fused_computation.127 | convolution fusion | flops 2415919104 | bytes 10223616 | tf_op jit(solution)/shard_map/td,fd->tf/dot_general | solution.py:112
  122.9 21.8 %all-gather.8.cloned.1.call-done = bf16[1024,768]{1,0:T(8,128)(2,1)} async-done(((bf16[1024,384]{1,0:T(8,128)(2,1)}), bf16[1024,768]{1,0:T(8,128)(2,1)}) %all-gather.8.cloned.1.call-update) | async-done | bytes 1572880 | tf_op jit(solution)/shard_map/all_gather | solution.py:97
  147.2 9.7 %fusion.6 = (bf16[1024,1536]{1,0:T(8,128)(2,1)S(1)}, f32[1024,1536]{1,0:T(8,128)}) fusion(f32[1024,1536]{1,0:T(8,128)} %fusion.92, bf16[768,1536]{1,0:T(8,128)(2,1)S(1)} %copy-done, bf16[1024,768]{1,0:T(8,128)(2,1)S(1)} %copy-done.7, f32[768]{0:T(1024)S(1)} %copy-done.30, f32[768]{0:T(1024)S(1)} %copy-done.27, f32[1024]{0:T(1024)S(1)} %add_rsqrt_fusion, ...), kind=kOutput, calls=%fused_computation.8 | convolution fusion | flops 2452094976 | bytes 19675136 | tf_op jit(solution)/shard_map/dot_general | solution.py:102
  158.6 4.3 fusion.93
  164.5 7.7 %convolution_convert_fusion.1 = bf16[1024,768]{1,0:T(8,128)(2,1)} fusion(bf16[1536,768]{1,0:T(8,128)(2,1)S(1)} %copy-done.29, f32[1024,1536]{1,0:T(8,128)} %get-tuple-element.56), kind=kOutput, calls=%fused_computation.60 | convolution fusion | flops 2430861312 | bytes 10223616 | tf_op jit(solution)/shard_map/dot_general | solution.py:105
  175.2 73.7 %all-reduce.5.cloned.1.call-done = f32[1024,768]{1,0:T(8,128)} async-done(((f32[1024,768]{1,0:T(8,128)}), f32[1024,768]{1,0:T(8,128)}) %all-reduce.5.cloned.1.call-update) | async-done | bytes 3145744 | tf_op jit(solution)/shard_map/psum | solution.py:118
  273.6 5.4 bitcast_convert_fusion
  279.2 6.6 %fusion.82 = f32[768,1536]{1,0:T(8,128)} fusion(bf16[1024,1536]{1,0:T(8,128)(2,1)} %copy-done.32, bf16[1024,768]{1,0:T(8,128)(2,1)S(1)} %copy-done.8, f32[768]{0:T(1024)S(1)} %copy-done.30, f32[768]{0:T(1024)S(1)} %copy-done.27, f32[1024]{0:T(1024)S(1)} %add_rsqrt_fusion, f32[1024]{0:T(1024)S(1)} %broadcast_multiply_fusion.4), kind=kOutput, calls=%fused_computation.121 | convolution fusion | flops 2420637696 | bytes 9451520 | tf_op jit(solution)/shard_map/td,tf->df/dot_general | solution.py:114
  285.8 9.4 %fusion.86 = f32[1536,768]{1,0:T(8,128)} fusion(bf16[1024,768]{1,0:T(8,128)(2,1)S(1)} %copy-done.17, f32[1024,1536]{1,0:T(8,128)} %get-tuple-element.56), kind=kOutput, calls=%fused_computation.123 | convolution fusion | flops 2430074880 | bytes 12582912 | tf_op jit(solution)/shard_map/tf,td->fd/dot_general | solution.py:111
  297.7 4.3 convolution_bitcast_fusion
  306.7 17.3 %all-gather.12.cloned.1.call-done = bf16[2048,768]{1,0:T(8,128)(2,1)} async-done(((bf16[1024,768]{1,0:T(8,128)(2,1)}), bf16[2048,768]{1,0:T(8,128)(2,1)}) %all-gather.12.cloned.1.call-update) | async-done | bytes 3145744 | tf_op jit(solution)/shard_map/all_gather | solution.py:164
  324.0 4.1 reduce_sum.156
  328.1 4.6 fusion.30
  332.7 64.3 %all-reduce = (f32[768]{0:T(1024)}, f32[768]{0:T(1024)}, f32[768]{0:T(1024)}, f32[768]{0:T(1024)}) all-reduce(f32[768]{0:T(1024)S(1)} %get-tuple-element.32, f32[768]{0:T(1024)S(1)} %get-tuple-element.37, f32[768]{0:T(1024)S(1)} %get-tuple-element.30, f32[768]{0:T(1024)S(1)} %get-tuple-element.35), channel_id=1, replica_groups=mesh['dp'=16,'head'=2] {'dp'}, use_global_device_ids=true, to_apply=%region_21.22 | all-reduce | flops 3072 | bytes 24576 | tf_op jit(solution)/shard_map/psum | solution.py:170
  397.0 3.8 fusion.36
  400.8 185.2 %all-reduce.7.cloned.1.call-done = (f32[3,768,384]{1,2,0:T(8,128)}, f32[384,768]{1,0:T(8,128)}, f32[768,1536]{1,0:T(8,128)}, f32[1536,768]{1,0:T(8,128)}) async-done(((f32[3,768,384]{1,2,0:T(8,128)}, f32[384,768]{1,0:T(8,128)}, f32[768,1536]{1,0:T(8,128)}, f32[1536,768]{1,0:T(8,128)}), (f32[3,768,384]{1,2,0:T(8,128)}, f32[384,768]{1,0:T(8,128)}, f32[768,1536]{1,0:T(8,128)}, ...) | async-done | bytes 14155792 | tf_op jit(solution)/shard_map/psum | solution.py:170
  586.0 5.2 copy.34
  592.3 5.5 copy.49
  (131 shorter events, 66.1 us)
Async XLA Ops:
  7.2 140.0 %copy-start = (bf16[768,1536]{1,0:T(8,128)(2,1)S(1)}, bf16[768,1536]{1,0:T(8,128)(2,1)}, u32[]{:S(2)}) copy-start(bf16[768,1536]{1,0:T(8,128)(2,1)} %param.20) | copy-start | bytes 7077892
  7.2 32.3 %all-gather.6.cloned.1.call-start = ((), (), s32[]{:S(2)}) async-start(), calls=%async_computation.2 | async-start | bytes 2359296 | tf_op jit(solution)/shard_map/all_gather | solution.py:70
  7.9 34.1 %copy-start.28 = (f32[768]{0:T(1024)S(1)}, f32[768]{0:T(1024)}, u32[]{:S(2)}) copy-start(f32[768]{0:T(1024)} %param.14) | copy-start | bytes 9220
  7.9 34.1 %copy-start.31 = (f32[768]{0:T(1024)S(1)}, f32[768]{0:T(1024)}, u32[]{:S(2)}) copy-start(f32[768]{0:T(1024)} %param.15) | copy-start | bytes 9220
  7.9 78.7 %reduce-scatter.7.cloned.1.call-start = ((), (), s32[]{:S(2)}) async-start(), calls=%async_computation.7 | async-start | bytes 2359296
  46.1 4.4 copy-start.15
  60.3 28.6 %copy-start.12 = (bf16[1024,384]{1,0:T(8,128)(2,1)S(1)}, bf16[1024,384]{1,0:T(8,128)(2,1)}, u32[]{:S(2)}) copy-start(bf16[1024,384]{1,0:T(8,128)(2,1)} %param.13) | copy-start | bytes 2359300
  60.4 55.1 %all-gather.10.cloned.1.call-start = ((), (), s32[]{:S(2)}) async-start(), calls=%async_computation.4 | async-start | bytes 2359296 | tf_op jit(solution)/shard_map/all_gather | solution.py:110
  61.1 83.5 %all-gather.8.cloned.1.call-start = ((), (), s32[]{:S(2)}) async-start(), calls=%async_computation.3 | async-start | bytes 2359296 | tf_op jit(solution)/shard_map/all_gather | solution.py:97
  91.2 157.7 %all-reduce.5.cloned.1.call-start = ((), (), s32[]{:S(2)}) async-start(), calls=%async_computation.5 | async-start | bytes 6291456 | tf_op jit(solution)/shard_map/psum | solution.py:118
  122.9 24.3 %copy-start.27 = (f32[768]{0:T(1024)S(1)}, f32[768]{0:T(1024)}, u32[]{:S(2)}) copy-start(f32[768]{0:T(1024)} %param.18) | copy-start | bytes 9220
  122.9 24.3 %copy-start.30 = (f32[768]{0:T(1024)S(1)}, f32[768]{0:T(1024)}, u32[]{:S(2)}) copy-start(f32[768]{0:T(1024)} %param.19) | copy-start | bytes 9220
  162.9 139.1 %reduce-scatter.9.cloned.1.call-start = ((), (), s32[]{:S(2)}) async-start(), calls=%async_computation.8 | async-start | bytes 2359296
  172.2 76.6 %copy-start.8 = (bf16[1024,768]{1,0:T(8,128)(2,1)S(1)}, bf16[1024,768]{1,0:T(8,128)(2,1)}, u32[]{:S(2)}) copy-start(bf16[1024,768]{1,0:T(8,128)(2,1)} %all-gather.8.cloned.1.call-done) | copy-start | bytes 4718596
  175.0 149.1 %all-gather.12.cloned.1.call-start = ((), (), s32[]{:S(2)}) async-start(), calls=%async_computation.6 | async-start | bytes 4718592 | tf_op jit(solution)/shard_map/all_gather | solution.py:164
  266.4 7.2 %copy-start.21 = (bf16[1,1024,384]{2,1,0:T(8,128)(2,1)S(1)}, bf16[1,1024,384]{2,1,0:T(8,128)(2,1)}, u32[]{:S(2)}) copy-start(bf16[1,1024,384]{2,1,0:T(8,128)(2,1)} %copy.32) | copy-start | bytes 2359300
  278.9 307.1 %all-reduce.7.cloned.1.call-start = ((), (), s32[]{:S(2)}) async-start(), calls=%async_computation.9 | async-start | bytes 28311552 | tf_op jit(solution)/shard_map/psum | solution.py:170
  279.2 6.6 %copy-start.17 = (bf16[1024,768]{1,0:T(8,128)(2,1)S(1)}, bf16[1024,768]{1,0:T(8,128)(2,1)}, u32[]{:S(2)}) copy-start(bf16[1024,768]{1,0:T(8,128)(2,1)} %all-gather.10.cloned.1.call-done) | copy-start | bytes 4718596
  285.8 9.4 %copy-start.6 = (f32[1024,768]{1,0:T(8,128)S(1)}, f32[1024,768]{1,0:T(8,128)}, u32[]{:S(2)}) copy-start(f32[1024,768]{1,0:T(8,128)} %copy-done.5) | copy-start | bytes 9437188
  285.8 9.4 %copy-start.19 = (bf16[6,64,1024]{2,1,0:T(8,128)(2,1)S(1)}, bf16[6,64,1024]{2,1,0:T(8,128)(2,1)}, u32[]{:S(2)}) copy-start(bf16[6,64,1024]{2,1,0:T(8,128)(2,1)} %fusion.40) | copy-start | bytes 2359300
  586.0 5.3 copy-start.18
  591.3 6.5 %slice-start = ((s8[4718592]{0:T(1024)(128)(4,1)}), s8[4194304]{0:T(1024)(128)(4,1)S(1)}, s32[]{:S(2)}) async-start(s8[4718592]{0:T(1024)(128)(4,1)} %bitcast.64), calls=%async_computation.10 | async-start | bytes 8388608
  592.3 5.5 slice-start.1
  592.3 7.7 %copy-start.1 = (bf16[768,1536]{1,0:T(8,128)(2,1)S(1)}, bf16[768,1536]{1,0:T(8,128)(2,1)}, u32[]{:S(2)}) copy-start(bf16[768,1536]{1,0:T(8,128)(2,1)} %param.20) | copy-start | bytes 7077892
  (19 other events, 39.0 us)
Sparse Core Ops, SparseCore 0:
  9.5 29.9 all-gather.5
  60.5 26.1 reduce-scatter.6
  88.2 27.1 all-gather.9
  117.4 27.1 all-gather.7
  163.0 85.7 all-reduce.4
  251.0 26.1 reduce-scatter.8
  279.1 44.8 all-gather.11
  329.2 256.8 all-reduce.6
